TPU v7x, 32 devices: a whole 2x2x4 slice. The times are simulated.
32 devices in a mesh: grp: 4 (over y, x), dev: 8 (over z, core).
Axes of the slice: x: 2, y: 2, z: 4, core: 2. Of those that a mesh axis runs over, the one named last changes fastest.
Arguments:
- embeddings: bfloat16 [262144, 256], P(('grp', 'dev'))
- prior_dist: float32 [262144], P(('grp', 'dev')), may hold values from 1 to 3
- seed_ids: int32 [6, 512], replicated, may hold values from 0 to 262143, as said below
Outputs:
- min_dist: float32 [262144], P(('grp', 'dev'))
- group_means: float32 [6, 4], P(None, 'grp')
Inputs may be any that keep to these rules, and one draw needn't show every extreme that they name: `seed_ids`: round r's ids all lie in the rows of group r mod 4, that is from (r mod 4) * 65536 to (r mod 4 + 1) * 65536 - 1; ids may repeat.
All inputs are finite; a program needn't handle non-finite values.
Results may differ from a plain program's by a relative error of at most 0.0003.
Values may be sent and summed in bfloat16 or wider, within the bound.
A program may use at most 64 MiB of HBM per device.

v0:
```python
import functools

import jax
import jax.numpy as jnp
from jax import lax
from jax.experimental import pallas as pl
from jax.experimental.pallas import tpu as pltpu
from jax.sharding import PartitionSpec as P

MESH = pl.DeviceIdType.MESH
LOAD_CHUNKS = 8
TILE = 256
WIDE = 2048
NT = (((1,), (1,)), ((), ()))


def split_square(x):
    square = jnp.square(x)
    high = square.astype(jnp.bfloat16)
    return high, (square - high.astype(jnp.float32)).astype(jnp.bfloat16)


def kernel(
    sizes, ids, prior, e_hbm, dist, means,
    e, ef, pick, out_half, own_half, pin, half, zin, cent, snb, hm, rn, part, parts,
    load_sem, p_sem, rs_sem, ag_sem, grp_sem, fwd_sem, mean_sem,
):
    groups, devs, rounds, seeds, rows, width = sizes
    chips = devs // 2
    half_rows = seeds // 2
    piece = half_rows // chips
    slots = (rounds + groups - 1) // groups
    g, d = lax.axis_index("grp"), lax.axis_index("dev")
    c, h = d // 2, d % 2
    partner = c * 2 + (1 - h)
    row_start = (g * devs + d) * rows
    chunk = rows // LOAD_CHUNKS

    def load(i):
        at = pl.ds(i * chunk, chunk)
        return pltpu.make_async_copy(e_hbm.at[at], e.at[at], load_sem.at[i])

    for i in range(LOAD_CHUNKS):
        load(i).start()

    barrier = pltpu.get_barrier_semaphore()
    for o in range(1, devs):
        pl.semaphore_signal(barrier, inc=1, device_id=(g, (d + o) % devs), device_id_type=MESH)

    def peer(o):
        total, base = 0, 1
        while base < groups:
            total = total + (((g // base) % 2 + (o // base) % 2) % 2) * base
            base *= 2
        return total

    for o in range(1, groups):
        pl.semaphore_signal(barrier, inc=1, device_id=(peer(o), d), device_id_type=MESH)

    for i in range(LOAD_CHUNKS):
        load(i).wait()

        @pl.loop(0, chunk // 256)
        def _(t):
            at = pl.ds(pl.multiple_of(i * chunk + t * 256, 256), 256)
            ef[at, :] = e[at, :].astype(jnp.float32)

    def gather(slot, which, dst):
        r = g + groups * slot

        @pl.loop(0, half_rows // 16)
        def _(b):
            for q in range(16):
                i = b * 16 + q
                offset = ids[r, which * half_rows + i] - row_start
                inside = (offset >= 0) & (offset < rows)
                row = ef[pl.ds(jnp.where(inside, offset, 0), 1), :]
                pick[pl.ds(i, 1), :] = jnp.where(inside, row, 0.0)

        dst[slot] = pick[0:half_rows, :].astype(jnp.bfloat16)

    def send(src, dst, sem, k, j, device):
        return pltpu.make_async_remote_copy(
            src_ref=src, dst_ref=dst, send_sem=sem.at[0, k, j], recv_sem=sem.at[1, k, j],
            device_id=device, device_id_type=MESH,
        )

    def to_partner(k):
        return send(out_half.at[k], pin.at[k], p_sem, k, 0, (g, partner))

    def scatter(k, o):
        target = (c + o) % chips
        return send(half.at[k, target], zin.at[k, o], rs_sem, k, o, (g, target * 2 + h))

    def spread(k, o):
        block = cent.at[g + groups * k, h, c]
        return send(block, block, ag_sem, k, o, (g, ((c + o) % chips) * 2 + h))

    def across(k, o, origin=None):
        block = cent.at[(g if origin is None else origin) + groups * k, h]
        return send(block, block, grp_sem, k, o, (peer(o), d))

    def forward(k, o):
        block = cent.at[peer(o) + groups * k, h]
        return send(block, block, fwd_sem, k, o, (g, partner))

    def if_held(k, o, f):
        if groups * (k + 1) <= rounds:
            f()
        else:
            pl.when(peer(o) + groups * k < rounds)(f)

    def start_slot(k):
        def f():
            gather(k, 1 - h, out_half)
            if k == 0:
                pl.semaphore_wait(barrier, devs - 1 + groups - 1)
            to_partner(k).start()
            gather(k, h, own_half)
            to_partner(k).wait_recv()
            both = own_half[k] + pin[k]
            half[k] = both.reshape(chips, piece, width)
            for o in range(1, chips):
                scatter(k, o).start()

        if_held(k, 0, f)

    for k in range(slots):
        start_slot(k)

    ones_row = jnp.ones((8, width), jnp.bfloat16)

    def row_norms(first, last):
        @pl.loop(first, last)
        def _(t):
            for j in range(WIDE // TILE):
                high, low = split_square(ef[pl.ds(pl.multiple_of(t * WIDE + j * TILE, TILE), TILE), :])
                total = lax.dot_general(ones_row, high, NT, preferred_element_type=jnp.float32)
                total += lax.dot_general(ones_row, low, NT, preferred_element_type=jnp.float32)
                for q in range(TILE // 128):
                    at = t * (WIDE // 128) + j * (TILE // 128) + q
                    rn[at] = total[:, q * 128 : (q + 1) * 128]

    def reduce_chips(k):
        def f():
            total = half[k, c]
            for o in range(1, chips):
                scatter(k, o).wait_recv()
                total += zin[k, o]
            cent[g + groups * k, h, c] = total
            for o in range(1, chips):
                spread(k, o).start()

        if_held(k, 0, f)

    def share(k):
        def f():
            for o in range(1, chips):
                spread(k, o).wait_recv()
            for o in range(1, groups):
                across(k, o).start()
            forward(k, 0).start()

        if_held(k, 0, f)

    steps = rows // WIDE
    parts_of = [steps * i // (slots + 1) for i in range(slots + 2)]
    for k in range(slots):
        row_norms(parts_of[k], parts_of[k + 1])
        reduce_chips(k)
    row_norms(parts_of[slots], steps)
    for k in range(slots):
        share(k)

    ones_col = jnp.ones((width, 128), jnp.bfloat16)

    def compute(r):
        centers = cent[r].reshape(seeds, width)
        high, low = split_square(centers.astype(jnp.float32))
        norms = jnp.dot(high, ones_col, preferred_element_type=jnp.float32)
        norms += jnp.dot(low, ones_col, preferred_element_type=jnp.float32)
        snb[...] = 0.5 * norms

        @pl.loop(0, rows // WIDE)
        def _(t):
            for j in range(WIDE // TILE):
                at = pl.multiple_of(t * WIDE + j * TILE, TILE)
                products = lax.dot_general(
                    cent[r].reshape(seeds, width), e[pl.ds(at, TILE), :], NT,
                    preferred_element_type=jnp.float32,
                )
                for q in range(TILE // 128):
                    score = products[:, q * 128 : (q + 1) * 128] - snb[...]
                    hm[r, t * (WIDE // 128) + j * (TILE // 128) + q] = jnp.max(
                        score.reshape(seeds // 8, 8, 128), axis=0
                    )

    items = [(k, 0) for k in range(slots)]
    items += [(k, o) for k in range(slots) for o in range(1, groups)]

    def relay(k, o):
        def f():
            across(k, o, peer(o)).wait_recv()
            forward(k, o).start()

        if o:
            if_held(k, o, f)

    def finish(k, o):
        def f():
            forward(k, o).wait_recv()
            compute(peer(o) + groups * k)

        if_held(k, o, f)

    for n, (k, o) in enumerate(items):
        if n == slots:
            relay(k, o)
        if n >= slots and n + 1 < len(items):
            relay(*items[n + 1])
        finish(k, o)

    current = prior[...]
    norms = jnp.max(rn[...], axis=1)
    sums = []
    for r in range(rounds):
        best = jnp.max(hm[r], axis=1)
        gap = jnp.maximum(norms - 2.0 * best, 0.0) * (1.0 / width)
        current = jnp.minimum(current, gap)
        sums.append(jnp.sum(current, axis=0, keepdims=True))
    if rounds < 8:
        sums.append(jnp.zeros((8 - rounds, 128), jnp.float32))
    part[...] = jnp.concatenate(sums, axis=0)
    dist[...] = current

    def send_part(o):
        return send(part, parts.at[o], mean_sem, 0, o, (g, (d + o) % devs))

    for o in range(1, devs):
        send_part(o).start()
    total = part[...]
    for o in range(1, devs):
        send_part(o).wait_recv()
        total += parts[o]
    means[...] = jnp.broadcast_to(
        jnp.sum(total, axis=1, keepdims=True) / float(rows * devs), (8, 128)
    )

    for o in range(1, devs):
        send_part(o).wait_send()
    for k in range(slots):
        def drain(k=k):
            to_partner(k).wait_send()
            for o in range(1, chips):
                scatter(k, o).wait_send()
                spread(k, o).wait_send()
            for o in range(1, groups):
                across(k, o).wait_send()

        if_held(k, 0, drain)
        for o in range(groups):
            if_held(k, o, lambda k=k, o=o: forward(k, o).wait_send())


def body(embeddings, prior_dist, seed_ids):
    rows, width = embeddings.shape
    rounds, seeds = seed_ids.shape
    groups, devs = lax.axis_size("grp"), lax.axis_size("dev")
    chips = devs // 2
    slots = (rounds + groups - 1) // groups
    half_rows = seeds // 2
    piece = half_rows // chips
    bf16, f32 = jnp.bfloat16, jnp.float32
    vmem = pl.BlockSpec(memory_space=pltpu.VMEM)
    dist, means = pl.pallas_call(
        functools.partial(kernel, (groups, devs, rounds, seeds, rows, width)),
        out_shape=(
            jax.ShapeDtypeStruct((rows // 128, 128), f32),
            jax.ShapeDtypeStruct((8, 128), f32),
        ),
        in_specs=[
            pl.BlockSpec(memory_space=pltpu.SMEM),
            vmem,
            pl.BlockSpec(memory_space=pl.ANY),
        ],
        out_specs=(vmem, vmem),
        scratch_shapes=[
            pltpu.VMEM((rows, width), bf16),
            pltpu.VMEM((rows + 8, width), f32),
            pltpu.VMEM((half_rows + 8, width), f32),
            pltpu.VMEM((slots, half_rows, width), bf16),
            pltpu.VMEM((slots, half_rows, width), bf16),
            pltpu.VMEM((slots, half_rows, width), bf16),
            pltpu.VMEM((slots, chips, piece, width), bf16),
            pltpu.VMEM((slots, chips, piece, width), bf16),
            pltpu.VMEM((rounds, 2, chips, piece, width), bf16),
            pltpu.VMEM((seeds, 128), f32),
            pltpu.VMEM((rounds, rows // 128, 8, 128), f32),
            pltpu.VMEM((rows // 128, 8, 128), f32),
            pltpu.VMEM((8, 128), f32),
            pltpu.VMEM((devs, 8, 128), f32),
            pltpu.SemaphoreType.DMA((LOAD_CHUNKS,)),
            pltpu.SemaphoreType.DMA((2, slots, 1)),
            pltpu.SemaphoreType.DMA((2, slots, chips)),
            pltpu.SemaphoreType.DMA((2, slots, chips)),
            pltpu.SemaphoreType.DMA((2, slots, groups)),
            pltpu.SemaphoreType.DMA((2, slots, groups)),
            pltpu.SemaphoreType.DMA((2, 1, devs)),
        ],
        compiler_params=pltpu.CompilerParams(
            collective_id=0, has_side_effects=True, vmem_limit_bytes=56 * 1024 * 1024
        ),
        name="seed_rounds",
    )(seed_ids, prior_dist.reshape(rows // 128, 128), embeddings)
    return dist.reshape(rows), means[:rounds, :1]


def solution(mesh):
    placed = (P(("grp", "dev"), None), P(("grp", "dev")), P())
    return jax.shard_map(
        body,
        mesh=mesh,
        in_specs=placed,
        out_specs=(P(("grp", "dev")), P(None, "grp")),
        check_vma=False,
    )
```

profile of v0, /device:TPU:0, one launch (start us, length us, event | category | flops | bytes accessed | tf_op | source)
XLA Modules:
  0.0 53.9 jit_solution(15776688996037846271)
XLA Ops:
  0.6 50.6 %seed_rounds.1 = (f32[64,128]{1,0:T(8,128)}, f32[8,128]{1,0:T(8,128)}) custom-call(s32[6,512]{1,0:T(8,128)} %ids.1, f32[64,128]{1,0:T(8,128)} %bitcast.3, bf16[8192,256]{1,0:T(8,128)(2,1)} %e_hbm.1), custom_call_target="tpu_custom_call" | custom-call | tf_op jit(solution)/shard_map/seed_rounds/pallas_call | solution.py:275
  51.2 1.3 %copy.5 = f32[6,1]{0,1:T(1,128)} copy(f32[6,1]{1,0:T(8,128)} %bitcast.5) | data formatting | bytes 48
  52.5 1.4 %copy.7 = f32[8192]{0:T(1024)} copy(f32[8192]{0:T(1024)} %bitcast.4) | data formatting | bytes 65536
where the time goes:
time: 54.7 us; the launch traced here: 53.9 us
  Pallas kernels  50.6 us (93%)
  local copies, waits for them, and re-layouts  2.64 us (5%)
  between operations  0.64 us (1%)
    pallas_call x1, Pallas kernels, body(): pl.pallas_call(functools.partial(kernel, (groups, devs, rounds, seeds, ro...  50.6 us
    unnamed x2, local copies, waits for them, and re-layouts  2.64 us

commit v1 on v0

v1 whole, which is shorter than its diff:
```python
import functools

import jax
import jax.numpy as jnp
from jax import lax
from jax.experimental import pallas as pl
from jax.experimental.pallas import tpu as pltpu
from jax.sharding import PartitionSpec as P

MESH = pl.DeviceIdType.MESH
LOAD_CHUNKS = 8
TILE = 256
NT = (((1,), (1,)), ((), ()))


def kernel(
    sizes, ids_hbm, prior_hbm, e_hbm, dist, means,
    ids, prior, e, ef, pick, out_half, own_half, pin, half, zin, cent, snb, near, rn, part, parts,
    ids_sem, prior_sem, load_sem, p_sem, rs_sem, ag_sem, grp_sem, fwd_sem, mean_sem,
):
    groups, devs, rounds, seeds, rows, width, subs = sizes
    chips = devs // 2
    sub = seeds // subs
    half_rows = sub // 2
    slots = (rounds + groups - 1) // groups
    wide = width // 2
    g, d = lax.axis_index("grp"), lax.axis_index("dev")
    c, h = d // 2, d % 2
    partner = c * 2 + (1 - h)
    row_start = (g * devs + d) * rows
    chunk = rows // LOAD_CHUNKS

    def load(i):
        at = pl.ds(i * chunk, chunk)
        return pltpu.make_async_copy(e_hbm.at[at], e.at[at], load_sem.at[i])

    load_ids = pltpu.make_async_copy(ids_hbm, ids, ids_sem)
    load_prior = pltpu.make_async_copy(prior_hbm, prior, prior_sem)
    for i in range(LOAD_CHUNKS):
        load(i).start()
    load_ids.start()
    load_prior.start()

    barrier = pltpu.get_barrier_semaphore()
    for o in range(1, devs):
        pl.semaphore_signal(barrier, inc=1, device_id=(g, (d + o) % devs), device_id_type=MESH)

    def peer(o):
        total, base = 0, 1
        while base < groups:
            total = total + (((g // base) % 2 + (o // base) % 2) % 2) * base
            base *= 2
        return total

    for o in range(1, groups):
        pl.semaphore_signal(barrier, inc=1, device_id=(peer(o), d), device_id_type=MESH)

    with jax.named_scope("loadconv"):
        ef[:, pl.ds(rows, 8), :] = jnp.zeros((2, 8, wide), jnp.float32)
        for i in range(LOAD_CHUNKS):
            load(i).wait()

            @pl.loop(0, chunk // 256)
            def _(t):
                at = pl.ds(pl.multiple_of(i * chunk + t * 256, 256), 256)
                for b in range(2):
                    ef[b, at, :] = e[at, b * wide : (b + 1) * wide].astype(jnp.float32)

        load_ids.wait()

    def gather(k, s, which, dst):
        with jax.named_scope("gather"):
            r = g + groups * k
            first = s * sub + which * half_rows

            @pl.loop(0, half_rows // 32)
            def _(b):
                for q in range(32):
                    i = b * 32 + q
                    offset = ids[r, first + i] - row_start
                    row = jnp.where((offset >= 0) & (offset < rows), offset, rows)
                    for w in range(2):
                        pick[w, pl.ds(i, 1), :] = ef[w, pl.ds(row, 1), :]

            u = k * subs + s
            for w in range(2):
                dst[u, :, w * wide : (w + 1) * wide] = pick[w].astype(jnp.bfloat16)

    def send(src, dst, sem, k, j, device):
        return pltpu.make_async_remote_copy(
            src_ref=src, dst_ref=dst, send_sem=sem.at[0, k, j], recv_sem=sem.at[1, k, j],
            device_id=device, device_id_type=MESH,
        )

    def block(owner, u):
        return cent.at[owner + groups * (u // subs), u % subs]

    def to_partner(u):
        return send(out_half.at[u], pin.at[u], p_sem, u, 0, (g, partner))

    def scatter(u, o):
        target = (c + o) % chips
        return send(half.at[u, target], zin.at[u, o], rs_sem, u, o, (g, target * 2 + h))

    def spread(u, o):
        ref = block(g, u).at[h, c]
        return send(ref, ref, ag_sem, u, o, (g, ((c + o) % chips) * 2 + h))

    def across(u, o, origin=None):
        ref = block(g if origin is None else origin, u).at[h]
        return send(ref, ref, grp_sem, u, o, (peer(o), d))

    def forward(u, o):
        ref = block(peer(o), u).at[h]
        return send(ref, ref, fwd_sem, u, o, (g, partner))

    def if_held(k, o, f):
        if isinstance(k, int) and groups * (k + 1) <= rounds:
            f()
        else:
            pl.when(peer(o) + groups * k < rounds)(f)

    def pair_sum(u):
        with jax.named_scope("pairsum"):
            to_partner(u).wait_recv()
            both = own_half[u] + pin[u]
            half[u] = both.reshape(half.shape[1:])
            for o in range(1, chips):
                scatter(u, o).start()

    def start_slot(k):
        def f():
            for s in range(subs):
                gather(k, s, 1 - h, out_half)
                if k == 0 and s == 0:
                    with jax.named_scope("barrier"):
                        pl.semaphore_wait(barrier, devs - 1 + groups - 1)
                to_partner(k * subs + s).start()
            for s in range(subs):
                gather(k, s, h, own_half)
            for s in range(subs):
                pair_sum(k * subs + s)

        if_held(k, 0, f)

    for k in range(slots):
        start_slot(k)

    ones_row = jnp.ones((8, width), jnp.bfloat16)

    def row_norms(first, last):
        with jax.named_scope("rownorm"):
            for j in range(first, last):
                at = pl.ds(j * TILE, TILE)
                square = jnp.square(ef[0, at, :]) + jnp.square(ef[1, at, :])
                high = square.astype(jnp.bfloat16)
                low = (square - high.astype(jnp.float32)).astype(jnp.bfloat16)
                both = jnp.concatenate([high, low], axis=1)
                total = lax.dot_general(ones_row, both, NT, preferred_element_type=jnp.float32)
                for q in range(TILE // 128):
                    rn[pl.ds(j * (TILE // 128) + q, 1), :] = total[0:1, q * 128 : (q + 1) * 128]

    def reduce_chips(u):
        def f():
            with jax.named_scope("reducechips"):
                total = half[u, c]
                for o in range(1, chips):
                    scatter(u, o).wait_recv()
                    total += zin[u, o]
                block(g, u)[h, c] = total
                for o in range(1, chips):
                    spread(u, o).start()

        if_held(u // subs, 0, f)

    def share(u):
        def f():
            with jax.named_scope("share"):
                for o in range(1, chips):
                    spread(u, o).wait_recv()
                forward(u, 0).start()
                for o in range(1, groups):
                    across(u, o).start()

        if_held(u // subs, 0, f)

    steps = rows // TILE
    cuts = [steps * i // 4 for i in range(5)]
    row_norms(cuts[0], cuts[1])
    reduce_chips(0)
    row_norms(cuts[1], cuts[2])
    for u in range(1, subs):
        reduce_chips(u)
    row_norms(cuts[2], cuts[3])
    for u in range(subs):
        share(u)
    for u in range(subs, slots * subs):
        reduce_chips(u)
    row_norms(cuts[3], cuts[4])

    def compute(r, read, count, first):
        centers = read()
        values = centers.astype(jnp.float32)
        norms = jnp.sum(values * values, axis=1, keepdims=True)
        snb[0:count, :] = jnp.broadcast_to(0.5 * norms, (count, 128))
        for j in range(rows // TILE):
            products = lax.dot_general(
                read(), e[pl.ds(j * TILE, TILE), :], NT, preferred_element_type=jnp.float32
            )
            for q in range(TILE // 128):
                score = products[:, q * 128 : (q + 1) * 128] - snb[0:count, :]
                best = jnp.max(score, axis=0, keepdims=True)
                at = pl.ds(j * (TILE // 128) + q, 1)
                near[r, at, :] = best if first else jnp.maximum(near[r, at, :], best)

    for s in range(subs):
        with jax.named_scope("waitfwd"):
            forward(s, 0).wait_recv()
        with jax.named_scope("computesub"):
            compute(g, lambda: cent[g, s].reshape(sub, width), sub, s == 0)
    for u in range(subs, slots * subs):
        share(u)

    own_items = slots - 1
    items = own_items + slots * (groups - 1)

    def item(i):
        j = i - own_items
        own = i < own_items
        return jnp.where(own, i + 1, j // (groups - 1)), jnp.where(own, 0, j % (groups - 1) + 1)

    def relay(k, o):
        for s in range(subs):
            across(k * subs + s, o, peer(o)).wait_recv()
            forward(k * subs + s, o).start()

    @pl.loop(0, items)
    def _(i):
        k, o = item(i)
        nk, no = item(i + 1)
        r = peer(o) + groups * k

        @pl.when((i + 1 < items) & (no > 0) & (peer(no) + groups * nk < rounds))
        def _():
            with jax.named_scope("relay"):
                relay(nk, no)

        @pl.when(r < rounds)
        def _():
            with jax.named_scope("waitfwd"):
                for s in range(subs):
                    forward(k * subs + s, o).wait_recv()
            with jax.named_scope("compute"):
                compute(r, lambda: cent[r].reshape(seeds, width), seeds, True)

    with jax.named_scope("final"):
        load_prior.wait()
        current = prior[...]
        norms = rn[...]
        sums = []
        for r in range(rounds):
            gap = jnp.maximum(norms - 2.0 * near[r], 0.0) * (1.0 / width)
            current = jnp.minimum(current, gap)
            sums.append(jnp.sum(current, axis=0, keepdims=True))
        if rounds < 8:
            sums.append(jnp.zeros((8 - rounds, 128), jnp.float32))
        part[...] = jnp.concatenate(sums, axis=0)
        dist[...] = current

    def send_part(o):
        return send(part, parts.at[o], mean_sem, 0, o, (g, (d + o) % devs))

    with jax.named_scope("means"):
        for o in range(1, devs):
            send_part(o).start()
        total = part[...]
        for o in range(1, devs):
            send_part(o).wait_recv()
            total += parts[o]
        means[...] = jnp.broadcast_to(
            jnp.sum(total, axis=1, keepdims=True) / float(rows * devs), (8, 128)
        )

    for o in range(1, devs):
        send_part(o).wait_send()
    for k in range(slots):
        def drain(k=k):
            for u in range(k * subs, (k + 1) * subs):
                to_partner(u).wait_send()
                for o in range(1, chips):
                    scatter(u, o).wait_send()
                    spread(u, o).wait_send()
                for o in range(1, groups):
                    across(u, o).wait_send()

        def drain_forward(k, o):
            for u in range(k * subs, (k + 1) * subs):
                forward(u, o).wait_send()

        if_held(k, 0, drain)
        for o in range(groups):
            if_held(k, o, functools.partial(drain_forward, k, o))


def body(embeddings, prior_dist, seed_ids):
    rows, width = embeddings.shape
    rounds, seeds = seed_ids.shape
    groups, devs = lax.axis_size("grp"), lax.axis_size("dev")
    chips = devs // 2
    slots = (rounds + groups - 1) // groups
    subs = 2 if seeds // 4 // chips >= 16 else 1
    units = slots * subs
    half_rows = seeds // subs // 2
    piece = half_rows // chips
    bf16, f32 = jnp.bfloat16, jnp.float32
    vmem = pl.BlockSpec(memory_space=pltpu.VMEM)
    hbm = pl.BlockSpec(memory_space=pl.ANY)
    dist, means = pl.pallas_call(
        functools.partial(kernel, (groups, devs, rounds, seeds, rows, width, subs)),
        out_shape=(
            jax.ShapeDtypeStruct((rows // 128, 128), f32),
            jax.ShapeDtypeStruct((8, 128), f32),
        ),
        in_specs=[hbm, hbm, hbm],
        out_specs=(vmem, vmem),
        scratch_shapes=[
            pltpu.SMEM((rounds, seeds), jnp.int32),
            pltpu.VMEM((rows // 128, 128), f32),
            pltpu.VMEM((rows, width), bf16),
            pltpu.VMEM((2, rows + 8, width // 2), f32),
            pltpu.VMEM((2, half_rows, width // 2), f32),
            pltpu.VMEM((units, half_rows, width), bf16),
            pltpu.VMEM((units, half_rows, width), bf16),
            pltpu.VMEM((units, half_rows, width), bf16),
            pltpu.VMEM((units, chips, piece, width), bf16),
            pltpu.VMEM((units, chips, piece, width), bf16),
            pltpu.VMEM((rounds, subs, 2, chips, piece, width), bf16),
            pltpu.VMEM((seeds, 128), f32),
            pltpu.VMEM((rounds, rows // 128, 128), f32),
            pltpu.VMEM((rows // 128, 128), f32),
            pltpu.VMEM((8, 128), f32),
            pltpu.VMEM((devs, 8, 128), f32),
            pltpu.SemaphoreType.DMA,
            pltpu.SemaphoreType.DMA,
            pltpu.SemaphoreType.DMA((LOAD_CHUNKS,)),
            pltpu.SemaphoreType.DMA((2, units, 1)),
            pltpu.SemaphoreType.DMA((2, units, chips)),
            pltpu.SemaphoreType.DMA((2, units, chips)),
            pltpu.SemaphoreType.DMA((2, units, groups)),
            pltpu.SemaphoreType.DMA((2, units, groups)),
            pltpu.SemaphoreType.DMA((2, 1, devs)),
        ],
        compiler_params=pltpu.CompilerParams(
            collective_id=0, has_side_effects=True, vmem_limit_bytes=56 * 1024 * 1024
        ),
        name="seed_rounds",
    )(seed_ids, prior_dist.reshape(rows // 128, 128), embeddings)
    return dist.reshape(rows), means[:rounds, :1]


def solution(mesh):
    placed = (P(("grp", "dev"), None), P(("grp", "dev")), P())
    return jax.shard_map(
        body,
        mesh=mesh,
        in_specs=placed,
        out_specs=(P(("grp", "dev")), P(None, "grp")),
        check_vma=False,
    )
```

time: 54.7 us -> 45.8 us (0.84); the launches traced: 53.9 us -> 45.6 us
  Pallas kernels: 50.6 us -> 42.3 us
    pallas_call x1, Pallas kernels: 50.6 us -> 42.3 us  [body(): pl.pallas_call(functools.partial(kernel, (groups, devs, rounds, seeds, ro...]
where the time goes in v1:
time: 45.8 us; the launch traced here: 45.6 us
  Pallas kernels  42.3 us (92%)
  local copies, waits for them, and re-layouts  2.64 us (6%)
  between operations  0.64 us (1%)
    pallas_call x1, Pallas kernels, body(): pl.pallas_call(functools.partial(kernel, (groups, devs, rounds, seeds, ro...  42.3 us
    unnamed x2, local copies, waits for them, and re-layouts  2.64 us

profile of v1, /device:TPU:0, one launch (start us, length us, event | category | flops | bytes accessed | tf_op | source)
XLA Modules:
  0.0 45.6 jit_solution(13041036831096736000)
XLA Ops:
  0.6 42.3 %seed_rounds.1 = (f32[64,128]{1,0:T(8,128)}, f32[8,128]{1,0:T(8,128)}) custom-call(s32[6,512]{1,0:T(8,128)} %ids_hbm.1, f32[64,128]{1,0:T(8,128)} %bitcast.3, bf16[8192,256]{1,0:T(8,128)(2,1)} %e_hbm.1), custom_call_target="tpu_custom_call" | custom-call | tf_op jit(solution)/shard_map/seed_rounds/pallas_call | solution.py:318
  42.9 1.3 %copy.5 = f32[6,1]{0,1:T(1,128)} copy(f32[6,1]{1,0:T(8,128)} %bitcast.5) | data formatting | bytes 48
  44.2 1.4 %copy.7 = f32[8192]{0:T(1024)} copy(f32[8192]{0:T(1024)} %bitcast.4) | data formatting | bytes 65536

commit v2 on v1

v2 whole, which is shorter than its diff:
```python
import functools

import jax
import jax.numpy as jnp
from jax import lax
from jax.experimental import pallas as pl
from jax.experimental.pallas import tpu as pltpu
from jax.sharding import PartitionSpec as P

MESH = pl.DeviceIdType.MESH
LOAD_CHUNKS = 8
TILE = 256
NT = (((1,), (1,)), ((), ()))


def kernel(
    sizes, ids_hbm, prior_hbm, e_hbm, dist, means,
    ids, ids_v, prior, e, ef, pick, out_half, own_half, pin, half, zin, cent, snb, near, rn, part, parts,
    ids_sem, rows_sem, prior_sem, load_sem, sent,
    p_sem, rs_sem, ag_sem, grp_sem, fwd_sem, mean_sem,
):
    groups, devs, rounds, seeds, rows, width, subs = sizes
    chips = devs // 2
    sub = seeds // subs
    half_rows = sub // 2
    slots = (rounds + groups - 1) // groups
    wide = width // 2
    g, d = lax.axis_index("grp"), lax.axis_index("dev")
    c, h = d // 2, d % 2
    owners, others = chips // 2, chips - chips // 2
    first_owner = chips // 4
    w = c - first_owner
    owns = (w >= 0) & (w < owners)
    partner = c * 2 + (1 - h)
    row_start = (g * devs + d) * rows
    chunk = rows // LOAD_CHUNKS

    def load(i):
        at = pl.ds(i * chunk, chunk)
        return pltpu.make_async_copy(e_hbm.at[at], e.at[at], load_sem.at[i])

    load_ids = pltpu.make_async_copy(ids_hbm, ids_v, ids_sem)
    set_ids = pltpu.make_async_copy(ids_v, ids, rows_sem)
    load_prior = pltpu.make_async_copy(prior_hbm, prior, prior_sem)
    load_ids.start()
    for i in range(LOAD_CHUNKS):
        load(i).start()
    load_prior.start()

    barrier = pltpu.get_barrier_semaphore()
    for o in range(1, devs):
        pl.semaphore_signal(barrier, inc=1, device_id=(g, (d + o) % devs), device_id_type=MESH)

    def peer(o):
        total, base = 0, 1
        while base < groups:
            total = total + (((g // base) % 2 + (o // base) % 2) % 2) * base
            base *= 2
        return total

    for o in range(1, groups):
        pl.semaphore_signal(barrier, inc=1, device_id=(peer(o), d), device_id_type=MESH)

    with jax.named_scope("loadconv"):
        load_ids.wait()
        offset = ids_v[...] - row_start
        ids_v[...] = jnp.where((offset >= 0) & (offset < rows), offset, rows)
        ef[:, pl.ds(rows, 8), :] = jnp.zeros((2, 8, wide), jnp.float32)

        @pl.loop(0, rounds)
        def _(r):
            near[r] = jnp.full(near.shape[1:], -1e38, jnp.float32)

        set_ids.start()
        for i in range(LOAD_CHUNKS):
            load(i).wait()

            @pl.loop(0, chunk // 256)
            def _(t):
                at = pl.ds(pl.multiple_of(i * chunk + t * 256, 256), 256)
                for b in range(2):
                    ef[b, at, :] = e[at, b * wide : (b + 1) * wide].astype(jnp.float32)

        set_ids.wait()

    def gather(k, s, which, dst):
        with jax.named_scope("gather"):
            r = g + groups * k
            first = s * sub + which * half_rows

            for i in range(half_rows):
                row = ids[r, first + i]
                for part_of in range(2):
                    pick[part_of, i : i + 1, :] = ef[part_of, pl.ds(row, 1), :]
            u = k * subs + s
            for part_of in range(2):
                at = slice(part_of * wide, (part_of + 1) * wide)
                dst[u, :, at] = pick[part_of].astype(jnp.bfloat16)

    PAIR, SCATTER, SPREAD, ACROSS, FORWARD = (n * slots * groups for n in range(5))
    MEAN = 5 * slots * groups

    def send(src, dst, send_sem, recv_sem, device):
        return pltpu.make_async_remote_copy(
            src_ref=src, dst_ref=dst, send_sem=send_sem, recv_sem=recv_sem,
            device_id=device, device_id_type=MESH,
        )

    def sent_sem(kind, u, q=0):
        return sent.at[kind + u // subs * groups + q]

    def wait_sent(kind, k, q, count):
        ref = e.at[pl.ds(0, count)]
        send(ref, ref, sent.at[kind + k * groups + q], mean_sem, (g, partner)).wait_send()

    def block(owner, u, half_index):
        return cent.at[owner + groups * (u // subs), half_index, u % subs]

    def to_partner(u):
        return send(out_half.at[u], pin.at[u], sent_sem(PAIR, u), p_sem.at[u], (g, partner))

    def scatter(u, target, slot):
        device = (g, (first_owner + target) * 2 + h)
        send_sem = sent_sem(SCATTER, u)
        return send(half.at[u, target], zin.at[u, slot], send_sem, rs_sem.at[u], device)

    def scatter_all(u):
        @pl.when(owns)
        def _():
            for o in range(1, owners):
                scatter(u, (w + o) % owners, o).start()

        @pl.when(jnp.logical_not(owns))
        def _():
            v = jnp.where(c < first_owner, c, c - owners)
            for target in range(owners):
                scatter(u, target, owners + v).start()

    def wait_scatter(u):
        ref = zin.at[u, pl.ds(1, chips - 1)]
        send(ref, ref, sent_sem(SCATTER, u), rs_sem.at[u], (g, partner)).wait_recv()

    def spread(u, o, q):
        ref = block(peer(q), u, h).at[w]
        device = (g, ((c + o) % chips) * 2 + h)
        return send(ref, ref, sent_sem(SPREAD, u, q), ag_sem.at[u, q], device)

    def wait_spread(u, q):
        def wait(count):
            ref = block(peer(q), u, h).at[pl.ds(0, count)]
            send(ref, ref, sent_sem(SPREAD, u, q), ag_sem.at[u, q], (g, partner)).wait_recv()

        if owners > 1:
            pl.when(owns)(functools.partial(wait, owners - 1))
        pl.when(jnp.logical_not(owns))(functools.partial(wait, owners))

    def by_piece(k, o, source):
        if k:
            return True
        twice = source + groups < rounds
        if o == 1:
            return jnp.logical_not(twice)
        return twice if o == groups - 1 else False

    def whole(k, o, source):
        piece = by_piece(k, o, source)
        return not piece if isinstance(piece, bool) else jnp.logical_not(piece)

    def only_if(condition, f):
        if condition is True:
            f()
        elif condition is not False:
            pl.when(condition)(f)

    def across(u, o, origin=None):
        ref = block(g if origin is None else origin, u, h)
        return send(ref, ref, sent_sem(ACROSS, u, o), grp_sem.at[u, o], (peer(o), d))

    def across_piece(u, o, origin=None):
        ref = block(g if origin is None else origin, u, h).at[w]
        return send(ref, ref, sent_sem(ACROSS, u, o), grp_sem.at[u, o], (peer(o), d))

    def forward(u, o):
        ref = block(peer(o), u, h)
        recv_sem = fwd_sem.at[u // subs * groups + o]
        return send(ref, ref, sent_sem(FORWARD, u, o), recv_sem, (g, partner))

    def wait_forward(k, o):
        with jax.named_scope("waitfwd"):
            ref = cent.at[peer(o) + groups * k, 1 - h]
            at = k * groups + o
            send(ref, ref, sent.at[FORWARD + at], fwd_sem.at[at], (g, partner)).wait_recv()

    def if_held(k, o, f):
        if groups * (k + 1) <= rounds:
            f()
        else:
            pl.when(peer(o) + groups * k < rounds)(f)

    def pair_sum(u):
        with jax.named_scope("pairsum"):
            to_partner(u).wait_recv()
            both = own_half[u] + pin[u]
            half[u] = both.reshape(half.shape[1:])

    def add_pair(u):
        if_held(u // subs, 0, functools.partial(pair_sum, u))

    def scatter_unit(u):
        if_held(u // subs, 0, lambda: scatter_all(u))

    def gather_out(u):
        def f():
            gather(u // subs, u % subs, 1 - h, out_half)
            if u == 0:
                with jax.named_scope("barrier"):
                    pl.semaphore_wait(barrier, devs - 1 + groups - 1)
            to_partner(u).start()

        if_held(u // subs, 0, f)

    def gather_own(u):
        if_held(u // subs, 0, lambda: gather(u // subs, u % subs, h, own_half))

    ones_row = jnp.ones((8, width), jnp.bfloat16)

    def row_norms(first, last):
        with jax.named_scope("rownorm"):
            for j in range(first, last):
                at = pl.ds(j * TILE, TILE)
                square = jnp.square(ef[0, at, :]) + jnp.square(ef[1, at, :])
                high = square.astype(jnp.bfloat16)
                low = (square - high.astype(jnp.float32)).astype(jnp.bfloat16)
                both = jnp.concatenate([high, low], axis=1)
                total = lax.dot_general(ones_row, both, NT, preferred_element_type=jnp.float32)
                for q in range(TILE // 128):
                    rn[pl.ds(j * (TILE // 128) + q, 1), :] = total[0:1, q * 128 : (q + 1) * 128]

    def reduce_chips(u):
        def f():
            with jax.named_scope("reduce%d" % u):
                wait_scatter(u)
                total = half[u, w]
                for slot in range(1, chips):
                    total += zin[u, slot]
                block(g, u, h)[w] = total
                for o in range(1, groups):
                    only_if(by_piece(u // subs, o, g), lambda: across_piece(u, o).start())
                for o in range(1, chips):
                    spread(u, o, 0).start()

        if_held(u // subs, 0, lambda: pl.when(owns)(f))

    def pass_piece(u, q):
        def f():
            with jax.named_scope("piece%d_%d" % (u, q)):
                across_piece(u, q, peer(q)).wait_recv()
                for o in range(1, chips):
                    spread(u, o, q).start()

        piece = by_piece(u // subs, q, peer(q))
        if_held(u // subs, q, lambda: only_if(piece, lambda: pl.when(owns)(f)))

    def share(u, q=0):
        def f():
            with jax.named_scope("share%d_%d" % (u, q)):
                k = u // subs
                if q:
                    only_if(by_piece(k, q, peer(q)), lambda: wait_spread(u, q))
                    only_if(whole(k, q, peer(q)), lambda: across(u, q, peer(q)).wait_recv())
                else:
                    wait_spread(u, 0)
                forward(u, q).start()
                if q == 0:
                    for o in range(1, groups):
                        only_if(whole(k, o, g), lambda: across(u, o).start())

        if_held(u // subs, q, f)

    steps = rows // TILE
    first_units = range(subs)
    late_units = range(subs, slots * subs)

    def start_units(units, scatter_now):
        gather_out(units[0])
        gather_own(units[0])
        for before, u in zip(units, units[1:]):
            gather_out(u)
            add_pair(before)
            if scatter_now:
                scatter_unit(before)
            gather_own(u)
        add_pair(units[-1])
        if scatter_now:
            scatter_unit(units[-1])

    start_units(first_units, True)
    if slots > 1:
        start_units(late_units, False)
    for u in first_units:
        reduce_chips(u)
    row_norms(0, steps // 2)
    for u in late_units:
        scatter_unit(u)
    row_norms(steps // 2, steps)
    for q in range(1, groups):
        for u in first_units:
            pass_piece(u, q)
    for u in first_units:
        share(u)

    def compute(r, read, count):
        centers = read()
        values = centers.astype(jnp.float32)
        norms = jnp.sum(values * values, axis=1, keepdims=True)
        snb[0:count, :] = jnp.broadcast_to(0.5 * norms, (count, 128))
        for j in range(rows // TILE):
            products = lax.dot_general(
                read(), e[pl.ds(j * TILE, TILE), :], NT, preferred_element_type=jnp.float32
            )
            for q in range(TILE // 128):
                score = products[:, q * 128 : (q + 1) * 128] - snb[0:count, :]
                best = jnp.max(score, axis=0, keepdims=True)
                at = pl.ds(j * (TILE // 128) + q, 1)
                near[r, at, :] = jnp.maximum(near[r, at, :], best)

    def item(i):
        return i // groups, i % groups

    halved = 3
    items = slots * groups

    def before_half(n):
        i, second = n // 2, n % 2
        if not second:
            if i:
                for u in first_units:
                    share(u, i)
            if i == 2:
                for u in late_units:
                    for q in range(1, groups):
                        pass_piece(u, q)
        else:
            if i == 0:
                for u in late_units:
                    reduce_chips(u)
            wait_forward(0, i)
            if i == halved - 1:
                for u in first_units:
                    share(u, halved)

    @pl.loop(0, 2 * halved)
    def _(n):
        for m in range(2 * halved):
            pl.when(n == m)(functools.partial(before_half, m))
        r = peer(n // 2)
        which = (h + n) % 2
        with jax.named_scope("half"):
            compute(r, lambda: cent[r, which].reshape(seeds // 2, width), seeds // 2)

    def before_item(i):
        if i + 1 < items:
            for s in range(subs):
                share((i + 1) // groups * subs + s, (i + 1) % groups)

    @pl.loop(halved, items)
    def _(i):
        k, o = item(i)
        r = peer(o) + groups * k
        for n in range(halved, items):
            pl.when(i == n)(functools.partial(before_item, n))

        @pl.when(r < rounds)
        def _():
            wait_forward(k, o)
            with jax.named_scope("compute"):
                compute(r, lambda: cent[r].reshape(seeds, width), seeds)

    with jax.named_scope("final"):
        load_prior.wait()
        current = prior[...]
        norms = rn[...]
        sums = []
        for r in range(rounds):
            gap = jnp.maximum(norms - 2.0 * near[r], 0.0) * (1.0 / width)
            current = jnp.minimum(current, gap)
            sums.append(jnp.sum(current, axis=0, keepdims=True))
        if rounds < 8:
            sums.append(jnp.zeros((8 - rounds, 128), jnp.float32))
        part[...] = jnp.concatenate(sums, axis=0)
        dist[...] = current

    def send_part(o):
        return send(part, parts.at[o], sent.at[MEAN], mean_sem, (g, (d + o) % devs))

    for o in range(1, devs):
        send_part(o).start()

    piece = half_rows // owners

    def drain(k, q):
        source = peer(q)
        wait_sent(FORWARD, k, q, subs * half_rows)
        if q == 0:
            wait_sent(PAIR, k, 0, subs * half_rows)
            if owners > 1:
                pl.when(owns)(lambda: wait_sent(SCATTER, k, 0, subs * (owners - 1) * piece))
            others_sent = subs * owners * piece
            pl.when(jnp.logical_not(owns))(lambda: wait_sent(SCATTER, k, 0, others_sent))
            for o in range(1, groups):
                only_if(
                    by_piece(k, o, g),
                    lambda: pl.when(owns)(lambda: wait_sent(ACROSS, k, o, subs * piece)),
                )
                only_if(whole(k, o, g), lambda: wait_sent(ACROSS, k, o, subs * half_rows))

        def spread_sent():
            wait_sent(SPREAD, k, q, subs * (chips - 1) * piece)

        only_if(True if q == 0 else by_piece(k, q, source), lambda: pl.when(owns)(spread_sent))

    with jax.named_scope("drain"):
        for k in range(slots):
            for q in range(groups):
                if_held(k, q, functools.partial(drain, k, q))

    with jax.named_scope("means"):
        total = part[...]
        every = parts.at[pl.ds(1, devs - 1)]
        means_in = send(every, every, sent.at[MEAN], mean_sem, (g, partner))
        means_in.wait_recv()
        for o in range(1, devs):
            total += parts[o]
        column = jnp.sum(total, axis=1, keepdims=True) / float(rows * devs)
        at_row = lax.broadcasted_iota(jnp.int32, (8, 128), 0)
        at_lane = lax.broadcasted_iota(jnp.int32, (8, 128), 1)
        line = jnp.sum(jnp.where(at_row == at_lane, column, 0.0), axis=0, keepdims=True)
        means[...] = jnp.broadcast_to(line, (8, 128))

    means_in.wait_send()


def emit(dist_in, means_in, dist, means):
    dist[...] = dist_in[...]
    means[...] = means_in[0:1, 0 : means.shape[1]]


def body(embeddings, prior_dist, seed_ids):
    rows, width = embeddings.shape
    rounds, seeds = seed_ids.shape
    groups, devs = lax.axis_size("grp"), lax.axis_size("dev")
    chips = devs // 2
    slots = (rounds + groups - 1) // groups
    subs = 2 if seeds // 4 // (chips // 2) >= 16 else 1
    units = slots * subs
    half_rows = seeds // subs // 2
    owners, others = chips // 2, chips - chips // 2
    piece = half_rows // owners
    bf16, f32 = jnp.bfloat16, jnp.float32
    vmem = pl.BlockSpec(memory_space=pltpu.VMEM)
    hbm = pl.BlockSpec(memory_space=pltpu.HBM)
    dist, means = pl.pallas_call(
        functools.partial(kernel, (groups, devs, rounds, seeds, rows, width, subs)),
        out_shape=(pltpu.VMEM((rows // 128, 128), f32), pltpu.VMEM((8, 128), f32)),
        in_specs=[hbm, hbm, hbm],
        out_specs=(vmem, vmem),
        scratch_shapes=[
            pltpu.SMEM((rounds, seeds), jnp.int32),
            pltpu.VMEM((rounds, seeds), jnp.int32),
            pltpu.VMEM((rows // 128, 128), f32),
            pltpu.VMEM((rows, width), bf16),
            pltpu.VMEM((2, rows + 8, width // 2), f32),
            pltpu.VMEM((2, half_rows, width // 2), f32),
            pltpu.VMEM((units, half_rows, width), bf16),
            pltpu.VMEM((units, half_rows, width), bf16),
            pltpu.VMEM((units, half_rows, width), bf16),
            pltpu.VMEM((units, owners, piece, width), bf16),
            pltpu.VMEM((units, owners + others, piece, width), bf16),
            pltpu.VMEM((rounds, 2, subs, owners, piece, width), bf16),
            pltpu.VMEM((seeds, 128), f32),
            pltpu.VMEM((rounds, rows // 128, 128), f32),
            pltpu.VMEM((rows // 128, 128), f32),
            pltpu.VMEM((8, 128), f32),
            pltpu.VMEM((devs, 8, 128), f32),
            pltpu.SemaphoreType.DMA,
            pltpu.SemaphoreType.DMA,
            pltpu.SemaphoreType.DMA,
            pltpu.SemaphoreType.DMA((LOAD_CHUNKS,)),
            pltpu.SemaphoreType.DMA((5 * slots * groups + 1,)),
            pltpu.SemaphoreType.DMA((units,)),
            pltpu.SemaphoreType.DMA((units,)),
            pltpu.SemaphoreType.DMA((units, groups)),
            pltpu.SemaphoreType.DMA((units, groups)),
            pltpu.SemaphoreType.DMA((slots * groups,)),
            pltpu.SemaphoreType.DMA,
        ],
        compiler_params=pltpu.CompilerParams(
            collective_id=0, has_side_effects=True, vmem_limit_bytes=56 * 1024 * 1024
        ),
        name="seed_rounds",
    )(seed_ids, prior_dist.reshape(rows // 128, 128), embeddings)
    dist, means = pl.pallas_call(
        emit,
        out_shape=(
            jax.ShapeDtypeStruct((rows // 128, 128), f32),
            jax.ShapeDtypeStruct((1, rounds), f32),
        ),
        in_specs=[vmem, vmem],
        out_specs=(vmem, vmem),
        compiler_params=pltpu.CompilerParams(vmem_limit_bytes=1024 * 1024),
        name="emit",
    )(dist, means)
    return dist.reshape(rows), means.reshape(rounds, 1)


def solution(mesh):
    placed = (P(("grp", "dev"), None), P(("grp", "dev")), P())
    return jax.shard_map(
        body,
        mesh=mesh,
        in_specs=placed,
        out_specs=(P(("grp", "dev")), P(None, "grp")),
        check_vma=False,
    )
```

time: 45.8 us -> 40.7 us (0.89)
  local copies, waits for them, and re-layouts: 2.64 us -> 0 us
  Pallas kernels: 42.3 us -> 39.9 us
    pallas_call x1, Pallas kernels: 42.3 us -> 39.3 us  [body(): pl.pallas_call(functools.partial(kernel, (groups, devs, rounds, seeds, ro...]
    unnamed x2 -> x0, local copies, waits for them, and re-layouts: 2.64 us -> none
    pallas_call x0 -> x1, Pallas kernels: none -> 0.62 us  [body(): pl.pallas_call(emit, out_shape=(jax.ShapeDtypeStruct((rows // 128, 128),...]
where the time goes in v2:
time: 40.7 us; the launch traced here: 40.5 us
  Pallas kernels  39.9 us (98%)
  between operations  0.64 us (2%)
    pallas_call x1, Pallas kernels, body(): pl.pallas_call(functools.partial(kernel, (groups, devs, rounds, seeds, ro...  39.3 us

profile of v2, /device:TPU:0, one launch (start us, length us, event | category | flops | bytes accessed | tf_op | source)
XLA Modules:
  0.0 40.5 jit_solution(758338801360612334)
XLA Ops:
  0.6 39.3 %seed_rounds.1 = (f32[64,128]{1,0:T(8,128)S(1)}, f32[8,128]{1,0:T(8,128)S(1)}) custom-call(s32[6,512]{1,0:T(8,128)} %ids_hbm.1, f32[64,128]{1,0:T(8,128)} %bitcast.3, bf16[8192,256]{1,0:T(8,128)(2,1)} %e_hbm.1), custom_call_target="tpu_custom_call" | custom-call | tf_op jit(solution)/shard_map/seed_rounds/pallas_call | solution.py:462
  39.9 0.6 %emit.1 = (f32[64,128]{1,0:T(8,128)}, f32[1,6]{1,0:T(1,128)}) custom-call(f32[64,128]{1,0:T(8,128)S(1)} %get-tuple-element.6.dist_in, f32[8,128]{1,0:T(8,128)S(1)} %get-tuple-element.7.means_in), custom_call_target="tpu_custom_call" | custom-call | tf_op jit(solution)/shard_map/emit/pallas_call | solution.py:502

commit v3 on v2

--- a/solution.py
+++ b/solution.py
@@ -15,8 +15,8 @@
 
 def kernel(
     sizes, ids_hbm, prior_hbm, e_hbm, dist, means,
-    ids, ids_v, prior, e, ef, pick, out_half, own_half, pin, half, zin, cent, snb, near, rn, part, parts,
-    ids_sem, rows_sem, prior_sem, load_sem, sent,
+    ids, prior, e, ef, pick, out_half, own_half, pin, half, zin, cent, snb, near, rn, part, parts,
+    ids_sem, prior_sem, load_sem, sent,
     p_sem, rs_sem, ag_sem, grp_sem, fwd_sem, mean_sem,
 ):
     groups, devs, rounds, seeds, rows, width, subs = sizes
@@ -30,6 +30,8 @@
     owners, others = chips // 2, chips - chips // 2
     first_owner = chips // 4
     w = c - first_owner
+    twice = g + groups < rounds
+    once = jnp.logical_not(twice)
     owns = (w >= 0) & (w < owners)
     partner = c * 2 + (1 - h)
     row_start = (g * devs + d) * rows
@@ -39,8 +41,7 @@
         at = pl.ds(i * chunk, chunk)
         return pltpu.make_async_copy(e_hbm.at[at], e.at[at], load_sem.at[i])
 
-    load_ids = pltpu.make_async_copy(ids_hbm, ids_v, ids_sem)
-    set_ids = pltpu.make_async_copy(ids_v, ids, rows_sem)
+    load_ids = pltpu.make_async_copy(ids_hbm, ids, ids_sem)
     load_prior = pltpu.make_async_copy(prior_hbm, prior, prior_sem)
     load_ids.start()
     for i in range(LOAD_CHUNKS):
@@ -62,16 +63,12 @@
         pl.semaphore_signal(barrier, inc=1, device_id=(peer(o), d), device_id_type=MESH)
 
     with jax.named_scope("loadconv"):
-        load_ids.wait()
-        offset = ids_v[...] - row_start
-        ids_v[...] = jnp.where((offset >= 0) & (offset < rows), offset, rows)
         ef[:, pl.ds(rows, 8), :] = jnp.zeros((2, 8, wide), jnp.float32)
 
         @pl.loop(0, rounds)
         def _(r):
             near[r] = jnp.full(near.shape[1:], -1e38, jnp.float32)
 
-        set_ids.start()
         for i in range(LOAD_CHUNKS):
             load(i).wait()
 
@@ -81,7 +78,7 @@
                 for b in range(2):
                     ef[b, at, :] = e[at, b * wide : (b + 1) * wide].astype(jnp.float32)
 
-        set_ids.wait()
+        load_ids.wait()
 
     def gather(k, s, which, dst):
         with jax.named_scope("gather"):
@@ -89,7 +86,7 @@
             first = s * sub + which * half_rows
 
             for i in range(half_rows):
-                row = ids[r, first + i]
+                row = jnp.minimum((ids[r, first + i] - row_start) & 0x7FFFFFFF, rows)
                 for part_of in range(2):
                     pick[part_of, i : i + 1, :] = ef[part_of, pl.ds(row, 1), :]
             u = k * subs + s
@@ -97,8 +94,8 @@
                 at = slice(part_of * wide, (part_of + 1) * wide)
                 dst[u, :, at] = pick[part_of].astype(jnp.bfloat16)
 
-    PAIR, SCATTER, SPREAD, ACROSS, FORWARD = (n * slots * groups for n in range(5))
-    MEAN = 5 * slots * groups
+    SPREAD, ACROSS, FORWARD = (n * slots * groups for n in range(3))
+    PAIR, SCATTER, MEAN = (3 * slots * groups + n * slots for n in range(3))
 
     def send(src, dst, send_sem, recv_sem, device):
         return pltpu.make_async_remote_copy(
@@ -107,11 +104,11 @@
         )
 
     def sent_sem(kind, u, q=0):
-        return sent.at[kind + u // subs * groups + q]
+        return sent.at[kind + u // subs * (groups if kind < PAIR else 1) + q]
 
     def wait_sent(kind, k, q, count):
         ref = e.at[pl.ds(0, count)]
-        send(ref, ref, sent.at[kind + k * groups + q], mean_sem, (g, partner)).wait_send()
+        send(ref, ref, sent_sem(kind, k * subs, q), mean_sem, (g, partner)).wait_send()
 
     def block(owner, u, half_index):
         return cent.at[owner + groups * (u // subs), half_index, u % subs]
@@ -157,10 +154,10 @@
     def by_piece(k, o, source):
         if k:
             return True
-        twice = source + groups < rounds
+        source_twice = source + groups < rounds
         if o == 1:
-            return jnp.logical_not(twice)
-        return twice if o == groups - 1 else False
+            return jnp.logical_not(source_twice)
+        return source_twice if o == 3 else False
 
     def whole(k, o, source):
         piece = by_piece(k, o, source)
@@ -271,9 +268,9 @@
                 else:
                     wait_spread(u, 0)
                 forward(u, q).start()
-                if q == 0:
-                    for o in range(1, groups):
-                        only_if(whole(k, o, g), lambda: across(u, o).start())
+                if u < subs and q == 0:
+                    pl.when(twice)(lambda: across(u, 1).start())
+                    pl.when(once)(lambda: across(u, 2).start())
 
         if_held(u // subs, q, f)
 
@@ -324,57 +321,70 @@
                 at = pl.ds(j * (TILE // 128) + q, 1)
                 near[r, at, :] = jnp.maximum(near[r, at, :], best)
 
-    def item(i):
-        return i // groups, i % groups
-
-    halved = 3
-    items = slots * groups
-
-    def before_half(n):
-        i, second = n // 2, n % 2
-        if not second:
-            if i:
-                for u in first_units:
-                    share(u, i)
-            if i == 2:
-                for u in late_units:
-                    for q in range(1, groups):
-                        pass_piece(u, q)
-        else:
-            if i == 0:
-                for u in late_units:
-                    reduce_chips(u)
-            wait_forward(0, i)
-            if i == halved - 1:
-                for u in first_units:
-                    share(u, halved)
-
-    @pl.loop(0, 2 * halved)
-    def _(n):
-        for m in range(2 * halved):
-            pl.when(n == m)(functools.partial(before_half, m))
-        r = peer(n // 2)
-        which = (h + n) % 2
-        with jax.named_scope("half"):
-            compute(r, lambda: cent[r, which].reshape(seeds // 2, width), seeds // 2)
-
-    def before_item(i):
-        if i + 1 < items:
-            for s in range(subs):
-                share((i + 1) // groups * subs + s, (i + 1) % groups)
-
-    @pl.loop(halved, items)
-    def _(i):
-        k, o = item(i)
-        r = peer(o) + groups * k
-        for n in range(halved, items):
-            pl.when(i == n)(functools.partial(before_item, n))
-
-        @pl.when(r < rounds)
-        def _():
+    def lag(u_list, q):
+        for u in u_list:
+            share(u, q)
+
+    def pieces_in(q):
+        for u in late_units:
+            pass_piece(u, q)
+
+    def late_pieces_out():
+        for u in late_units:
+            reduce_chips(u)
+        for u in first_units:
+            across(u, 2).start()
+
+    def diagonal_out():
+        for u in first_units:
+            across(u, 3).start()
+
+    HALF, REST, FULL = range(3)
+    kinds = [HALF, REST, HALF, REST, HALF, REST, FULL, HALF, REST, FULL]
+    two = [
+        (0, 0, []),
+        (0, 0, [late_pieces_out]),
+        (0, 2, [lambda: lag(first_units, 2)]),
+        (0, 2, []),
+        (0, 1, [lambda: lag(first_units, 1), lambda: pieces_in(1)]),
+        (0, 1, [lambda: lag(late_units, 0)]),
+        (1, 0, []),
+        (0, 3, [lambda: lag(first_units, 3)]),
+        (0, 3, [lambda: lag(late_units, 1)]),
+        (1, 1, []),
+    ]
+    one = [
+        (0, 0, []),
+        (0, 0, []),
+        (0, 1, [lambda: lag(first_units, 1), diagonal_out]),
+        (0, 1, []),
+        (0, 3, [lambda: lag(first_units, 3), lambda: pieces_in(2)]),
+        (0, 3, [lambda: lag(first_units, 2), lambda: pieces_in(3)]),
+        (0, 2, []),
+        (1, 2, [lambda: lag(late_units, 2)]),
+        (1, 2, [lambda: lag(late_units, 3)]),
+        (1, 3, []),
+    ]
+
+    def prepare(kind, k, o, actions):
+        for action in actions:
+            action()
+        if kind != HALF:
             wait_forward(k, o)
+
+    for kind, line_two, line_one in zip(kinds, two, one):
+        pl.when(twice)(functools.partial(prepare, kind, *line_two))
+        pl.when(once)(functools.partial(prepare, kind, *line_one))
+        r = jnp.where(
+            twice, peer(line_two[1]) + groups * line_two[0], peer(line_one[1]) + groups * line_one[0]
+        )
+        if kind == FULL:
             with jax.named_scope("compute"):
                 compute(r, lambda: cent[r].reshape(seeds, width), seeds)
+        else:
+            which = h if kind == HALF else 1 - h
+            with jax.named_scope("half"):
+                compute(r, lambda: cent[r, which].reshape(seeds // 2, width), seeds // 2)
 
     with jax.named_scope("final"):
         load_prior.wait()
@@ -466,7 +476,6 @@
         out_specs=(vmem, vmem),
         scratch_shapes=[
             pltpu.SMEM((rounds, seeds), jnp.int32),
-            pltpu.VMEM((rounds, seeds), jnp.int32),
             pltpu.VMEM((rows // 128, 128), f32),
             pltpu.VMEM((rows, width), bf16),
             pltpu.VMEM((2, rows + 8, width // 2), f32),
@@ -484,9 +493,8 @@
             pltpu.VMEM((devs, 8, 128), f32),
             pltpu.SemaphoreType.DMA,
             pltpu.SemaphoreType.DMA,
-            pltpu.SemaphoreType.DMA,
             pltpu.SemaphoreType.DMA((LOAD_CHUNKS,)),
-            pltpu.SemaphoreType.DMA((5 * slots * groups + 1,)),
+            pltpu.SemaphoreType.DMA((3 * slots * groups + 2 * slots + 1,)),
             pltpu.SemaphoreType.DMA((units,)),
             pltpu.SemaphoreType.DMA((units,)),
             pltpu.SemaphoreType.DMA((units, groups)),

time: 40.7 us -> 39.2 us (0.963)
  Pallas kernels: 39.9 us -> 38.4 us
    pallas_call x1, Pallas kernels: 39.3 us -> 37.8 us  [body(): pl.pallas_call(functools.partial(kernel, (groups, devs, rounds, seeds, ro...]
where the time goes in v3:
time: 39.2 us; the launch traced here: 39.1 us
  Pallas kernels  38.4 us (98%)
  between operations  0.64 us (2%)
    pallas_call x1, Pallas kernels, body(): pl.pallas_call(functools.partial(kernel, (groups, devs, rounds, seeds, ro...  37.8 us

profile of v3, /device:TPU:0, one launch (start us, length us, event | category | flops | bytes accessed | tf_op | source)
XLA Modules:
  0.0 39.1 jit_solution(13252284203239021195)
XLA Ops:
  0.6 37.8 %seed_rounds.1 = (f32[64,128]{1,0:T(8,128)S(1)}, f32[8,128]{1,0:T(8,128)S(1)}) custom-call(s32[6,512]{1,0:T(8,128)} %ids_hbm.1, f32[64,128]{1,0:T(8,128)} %bitcast.3, bf16[8192,256]{1,0:T(8,128)(2,1)} %e_hbm.1), custom_call_target="tpu_custom_call" | custom-call | tf_op jit(solution)/shard_map/seed_rounds/pallas_call | solution.py:472
  38.5 0.6 %emit.1 = (f32[64,128]{1,0:T(8,128)}, f32[1,6]{1,0:T(1,128)}) custom-call(f32[64,128]{1,0:T(8,128)S(1)} %get-tuple-element.6.dist_in, f32[8,128]{1,0:T(8,128)S(1)} %get-tuple-element.7.means_in), custom_call_target="tpu_custom_call" | custom-call | tf_op jit(solution)/shard_map/emit/pallas_call | solution.py:510

commit v4 on v3

--- a/solution.py
+++ b/solution.py
@@ -8,7 +8,7 @@
 from jax.sharding import PartitionSpec as P
 
 MESH = pl.DeviceIdType.MESH
-LOAD_CHUNKS = 8
+LOAD_CHUNKS = 4
 TILE = 256
 NT = (((1,), (1,)), ((), ()))
 
@@ -94,8 +94,7 @@
                 at = slice(part_of * wide, (part_of + 1) * wide)
                 dst[u, :, at] = pick[part_of].astype(jnp.bfloat16)
 
-    SPREAD, ACROSS, FORWARD = (n * slots * groups for n in range(3))
-    PAIR, SCATTER, MEAN = (3 * slots * groups + n * slots for n in range(3))
+    SPREAD, ACROSS, FORWARD, PAIR, SCATTER, MEAN = range(6)
 
     def send(src, dst, send_sem, recv_sem, device):
         return pltpu.make_async_remote_copy(
@@ -103,22 +102,20 @@
             device_id=device, device_id_type=MESH,
         )
 
-    def sent_sem(kind, u, q=0):
-        return sent.at[kind + u // subs * (groups if kind < PAIR else 1) + q]
-
-    def wait_sent(kind, k, q, count):
-        ref = e.at[pl.ds(0, count)]
-        send(ref, ref, sent_sem(kind, k * subs, q), mean_sem, (g, partner)).wait_send()
+    def wait_sent(kind, count):
+        if count:
+            ref = e.at[pl.ds(0, count)]
+            send(ref, ref, sent.at[kind], mean_sem, (g, partner)).wait_send()
 
     def block(owner, u, half_index):
         return cent.at[owner + groups * (u // subs), half_index, u % subs]
 
     def to_partner(u):
-        return send(out_half.at[u], pin.at[u], sent_sem(PAIR, u), p_sem.at[u], (g, partner))
+        return send(out_half.at[u], pin.at[u], sent.at[PAIR], p_sem.at[u], (g, partner))
 
     def scatter(u, target, slot):
         device = (g, (first_owner + target) * 2 + h)
-        send_sem = sent_sem(SCATTER, u)
+        send_sem = sent.at[SCATTER]
         return send(half.at[u, target], zin.at[u, slot], send_sem, rs_sem.at[u], device)
 
     def scatter_all(u):
@@ -135,17 +132,19 @@
 
     def wait_scatter(u):
         ref = zin.at[u, pl.ds(1, chips - 1)]
-        send(ref, ref, sent_sem(SCATTER, u), rs_sem.at[u], (g, partner)).wait_recv()
+        send(ref, ref, sent.at[SCATTER], rs_sem.at[u], (g, partner)).wait_recv()
 
     def spread(u, o, q):
         ref = block(peer(q), u, h).at[w]
-        device = (g, ((c + o) % chips) * 2 + h)
-        return send(ref, ref, sent_sem(SPREAD, u, q), ag_sem.at[u, q], device)
+        v = o - owners
+        other = v + jnp.where(v < first_owner, 0, owners) if o >= owners else (w + o) % owners + first_owner
+        device = (g, other * 2 + h)
+        return send(ref, ref, sent.at[SPREAD], ag_sem.at[u, q], device)
 
     def wait_spread(u, q):
         def wait(count):
             ref = block(peer(q), u, h).at[pl.ds(0, count)]
-            send(ref, ref, sent_sem(SPREAD, u, q), ag_sem.at[u, q], (g, partner)).wait_recv()
+            send(ref, ref, sent.at[SPREAD], ag_sem.at[u, q], (g, partner)).wait_recv()
 
         if owners > 1:
             pl.when(owns)(functools.partial(wait, owners - 1))
@@ -171,22 +170,22 @@
 
     def across(u, o, origin=None):
         ref = block(g if origin is None else origin, u, h)
-        return send(ref, ref, sent_sem(ACROSS, u, o), grp_sem.at[u, o], (peer(o), d))
+        return send(ref, ref, sent.at[ACROSS], grp_sem.at[u, o], (peer(o), d))
 
     def across_piece(u, o, origin=None):
         ref = block(g if origin is None else origin, u, h).at[w]
-        return send(ref, ref, sent_sem(ACROSS, u, o), grp_sem.at[u, o], (peer(o), d))
+        return send(ref, ref, sent.at[ACROSS], grp_sem.at[u, o], (peer(o), d))
 
     def forward(u, o):
         ref = block(peer(o), u, h)
         recv_sem = fwd_sem.at[u // subs * groups + o]
-        return send(ref, ref, sent_sem(FORWARD, u, o), recv_sem, (g, partner))
+        return send(ref, ref, sent.at[FORWARD], recv_sem, (g, partner))
 
     def wait_forward(k, o):
         with jax.named_scope("waitfwd"):
             ref = cent.at[peer(o) + groups * k, 1 - h]
             at = k * groups + o
-            send(ref, ref, sent.at[FORWARD + at], fwd_sem.at[at], (g, partner)).wait_recv()
+            send(ref, ref, sent.at[FORWARD], fwd_sem.at[at], (g, partner)).wait_recv()
 
     def if_held(k, o, f):
         if groups * (k + 1) <= rounds:
@@ -297,7 +296,7 @@
     for u in first_units:
         reduce_chips(u)
     row_norms(0, steps // 2)
-    for u in late_units:
+    for u in late_units[:1]:
         scatter_unit(u)
     row_norms(steps // 2, steps)
     for q in range(1, groups):
@@ -305,6 +304,9 @@
             pass_piece(u, q)
     for u in first_units:
         share(u)
+        if u == 0:
+            for v in late_units[1:]:
+                scatter_unit(v)
 
     def compute(r, read, count):
         centers = read()
@@ -330,27 +332,32 @@
             pass_piece(u, q)
 
     def late_pieces_out():
-        for u in late_units:
+        for u in late_units[:1]:
             reduce_chips(u)
         for u in first_units:
             across(u, 2).start()
 
+    def rest_out():
+        for u in late_units[1:]:
+            reduce_chips(u)
+
     def diagonal_out():
         for u in first_units:
             across(u, 3).start()
 
     HALF, REST, FULL = range(3)
-    kinds = [HALF, REST, HALF, REST, HALF, REST, FULL, HALF, REST, FULL]
+    two_kinds = [HALF, REST, HALF, REST, HALF, REST, FULL, FULL, None, FULL]
+    one_kinds = [HALF, REST, HALF, REST, HALF, REST, FULL, HALF, REST, FULL]
     two = [
         (0, 0, []),
         (0, 0, [late_pieces_out]),
-        (0, 2, [lambda: lag(first_units, 2)]),
+        (0, 2, [lambda: lag(first_units, 2), rest_out]),
         (0, 2, []),
         (0, 1, [lambda: lag(first_units, 1), lambda: pieces_in(1)]),
         (0, 1, [lambda: lag(late_units, 0)]),
-        (1, 0, []),
-        (0, 3, [lambda: lag(first_units, 3)]),
+        (1, 0, [lambda: lag(first_units, 3)]),
         (0, 3, [lambda: lag(late_units, 1)]),
+        None,
         (1, 1, []),
     ]
     one = [
@@ -372,12 +379,10 @@
         if kind != HALF:
             wait_forward(k, o)
 
-    for kind, line_two, line_one in zip(kinds, two, one):
-        pl.when(twice)(functools.partial(prepare, kind, *line_two))
-        pl.when(once)(functools.partial(prepare, kind, *line_one))
-        r = jnp.where(
-            twice, peer(line_two[1]) + groups * line_two[0], peer(line_one[1]) + groups * line_one[0]
-        )
+    def round_of(line):
+        return peer(line[1]) + groups * line[0]
+
+    def run(kind, r):
         if kind == FULL:
             with jax.named_scope("compute"):
                 compute(r, lambda: cent[r].reshape(seeds, width), seeds)
@@ -385,6 +390,20 @@
             which = h if kind == HALF else 1 - h
             with jax.named_scope("half"):
                 compute(r, lambda: cent[r, which].reshape(seeds // 2, width), seeds // 2)
+
+    def step(kind, line):
+        prepare(kind, *line)
+        run(kind, round_of(line))
+
+    for kind_two, kind_one, line_two, line_one in zip(two_kinds, one_kinds, two, one):
+        if kind_two == kind_one:
+            pl.when(twice)(functools.partial(prepare, kind_two, *line_two))
+            pl.when(once)(functools.partial(prepare, kind_one, *line_one))
+            run(kind_two, jnp.where(twice, round_of(line_two), round_of(line_one)))
+        else:
+            if line_two is not None:
+                pl.when(twice)(functools.partial(step, kind_two, line_two))
+            pl.when(once)(functools.partial(step, kind_one, line_one))
 
     with jax.named_scope("final"):
         load_prior.wait()
@@ -408,31 +427,32 @@
 
     piece = half_rows // owners
 
-    def drain(k, q):
-        source = peer(q)
-        wait_sent(FORWARD, k, q, subs * half_rows)
-        if q == 0:
-            wait_sent(PAIR, k, 0, subs * half_rows)
-            if owners > 1:
-                pl.when(owns)(lambda: wait_sent(SCATTER, k, 0, subs * (owners - 1) * piece))
-            others_sent = subs * owners * piece
-            pl.when(jnp.logical_not(owns))(lambda: wait_sent(SCATTER, k, 0, others_sent))
-            for o in range(1, groups):
-                only_if(
-                    by_piece(k, o, g),
-                    lambda: pl.when(owns)(lambda: wait_sent(ACROSS, k, o, subs * piece)),
-                )
-                only_if(whole(k, o, g), lambda: wait_sent(ACROSS, k, o, subs * half_rows))
-
-        def spread_sent():
-            wait_sent(SPREAD, k, q, subs * (chips - 1) * piece)
-
-        only_if(True if q == 0 else by_piece(k, q, source), lambda: pl.when(owns)(spread_sent))
+    def cut_up(k, o, source_twice):
+        return k > 0 or (not source_twice if o == 1 else source_twice and o == 3)
+
+    def drain(is_two, is_owner):
+        held = range(2 if is_two else 1)
+        half_unit, own_part = subs * half_rows, subs * piece
+        wait_sent(FORWARD, rounds * half_unit)
+        wait_sent(PAIR, len(held) * half_unit)
+        wait_sent(SCATTER, len(held) * own_part * (owners - 1 if is_owner else owners))
+        crossed, spreads = 0, 0
+        for k in range(2):
+            for o in range(groups):
+                source_two = is_two if o < 2 else not is_two
+                if k in held and o:
+                    in_pieces = cut_up(k, o, is_two)
+                    crossed += (own_part if is_owner else 0) if in_pieces else half_unit
+                if (k == 0 or source_two) and (o == 0 or cut_up(k, o, source_two)):
+                    spreads += own_part * (chips - 1)
+        wait_sent(ACROSS, crossed)
+        wait_sent(SPREAD, spreads if is_owner else 0)
 
     with jax.named_scope("drain"):
-        for k in range(slots):
-            for q in range(groups):
-                if_held(k, q, functools.partial(drain, k, q))
+        for is_two in (True, False):
+            for is_owner in (True, False):
+                mine = (twice if is_two else once) & (owns if is_owner else jnp.logical_not(owns))
+                pl.when(mine)(functools.partial(drain, is_two, is_owner))
 
     with jax.named_scope("means"):
         total = part[...]
@@ -494,7 +514,7 @@
             pltpu.SemaphoreType.DMA,
             pltpu.SemaphoreType.DMA,
             pltpu.SemaphoreType.DMA((LOAD_CHUNKS,)),
-            pltpu.SemaphoreType.DMA((3 * slots * groups + 2 * slots + 1,)),
+            pltpu.SemaphoreType.DMA((6,)),
             pltpu.SemaphoreType.DMA((units,)),
             pltpu.SemaphoreType.DMA((units,)),
             pltpu.SemaphoreType.DMA((units, groups)),

time: 39.2 us -> 38.9 us (level)
  no operation moved by 1% of the time
where the time goes in v4:
time: 38.9 us; the launch traced here: 38.8 us
  Pallas kernels  38.1 us (98%)
  between operations  0.64 us (2%)
    pallas_call x1, Pallas kernels, body(): pl.pallas_call(functools.partial(kernel, (groups, devs, rounds, seeds, ro...  37.5 us

profile of v4, /device:TPU:0, one launch (start us, length us, event | category | flops | bytes accessed | tf_op | source)
XLA Modules:
  0.0 38.8 jit_solution(16596728040119128137)
XLA Ops:
  0.6 37.5 %seed_rounds.1 = (f32[64,128]{1,0:T(8,128)S(1)}, f32[8,128]{1,0:T(8,128)S(1)}) custom-call(s32[6,512]{1,0:T(8,128)} %ids_hbm.1, f32[64,128]{1,0:T(8,128)} %bitcast.3, bf16[8192,256]{1,0:T(8,128)(2,1)} %e_hbm.1), custom_call_target="tpu_custom_call" | custom-call | tf_op jit(solution)/shard_map/seed_rounds/pallas_call | solution.py:492
  38.1 0.6 %emit.1 = (f32[64,128]{1,0:T(8,128)}, f32[1,6]{1,0:T(1,128)}) custom-call(f32[64,128]{1,0:T(8,128)S(1)} %get-tuple-element.6.dist_in, f32[8,128]{1,0:T(8,128)S(1)} %get-tuple-element.7.means_in), custom_call_target="tpu_custom_call" | custom-call | tf_op jit(solution)/shard_map/emit/pallas_call | solution.py:530
